TPU v7x, 128 devices: a whole 4x4x4 slice. The times are simulated.
128 devices in a mesh: member: 16 (over z, x_lo, core), space: 8 (over x_hi, y).
Axes of the slice: x: 4 (x_hi: 2, x_lo: 2; x = x_hi * 2 + x_lo), y: 4, z: 4, core: 2. Of those that a mesh axis runs over, the one named last changes fastest.
Arguments:
- weather: bfloat16 [16, 84, 256, 1440], P('member', None, 'space'), may hold values from -6 to 6
- coefficients: int32 [16, 84, 2, 368, 361], P('member', None, None, 'space'), may hold values from -1073741824 to 1073741823
- channel_scale: float32 [84], replicated, may hold values from 0.3 to 3
Outputs:
- perturbed: bfloat16 [16, 84, 256, 1440], P('member', None, 'space')
All inputs are finite; a program needn't handle non-finite values.
Results may differ from a plain program's by a relative error of at most 0.007.
Values may be sent and summed in bfloat16 or wider, within the bound.
A program may use at most 192 MiB of HBM per device.

v0:
```python
import math

import jax
import jax.numpy as jnp
from jax import lax
from jax.sharding import PartitionSpec as P


def in_blocks(array, dim, devices):
    lengths = array.shape
    parts = array.reshape(*lengths[:dim], devices, lengths[dim] // devices, *lengths[dim + 1 :])
    return jnp.moveaxis(parts, dim, 0)


def joined_along(parts, dim):
    lengths = list(parts.shape[1:])
    lengths[dim] *= parts.shape[0]
    return jnp.moveaxis(parts, 0, dim).reshape(lengths)


def exchange_both(array, axis, axes, splits, concats):
    sizes = [lax.axis_size(a) for a in axes]
    parts = in_blocks(array, splits[0], sizes[0])
    parts = jnp.moveaxis(in_blocks(parts, splits[1] + 1, sizes[1]), 0, 1)
    inside = parts.shape[2:]
    parts = parts.reshape(-1, *inside)
    parts = lax.all_to_all(parts, axis, split_axis=0, concat_axis=0, tiled=True)
    parts = joined_along(parts.reshape(*sizes, *inside), concats[0] + 1)
    return joined_along(parts, concats[1])


def diagonal_log(order_count):
    steps_up = jnp.arange(1, order_count, dtype=jnp.int32).astype(jnp.float32)
    terms = 0.5 * jnp.log((2.0 * steps_up + 1.0) / (2.0 * steps_up))
    return jnp.concatenate([jnp.zeros((1,), jnp.float32), jnp.cumsum(terms)])


def legendre_table(orders, colatitude, order_logs, degree_count):
    order_values = orders.astype(jnp.float32)[:, None]
    cosine = jnp.cos(colatitude)[None, :]
    sine_values = jnp.sin(colatitude)[None, :]
    diagonal = jnp.exp(
        order_logs[:, None] - 0.5 * math.log(4.0 * math.pi) + order_values * jnp.log(sine_values)
    )
    block_size = 16
    turn_count = (degree_count + block_size - 1) // block_size
    order_square = order_values * order_values

    def advance(carry, turn_index):
        older_row, newer_row = carry
        produced = []
        for inner_step in range(block_size):
            degree = (turn_index * block_size + inner_step).astype(jnp.float32)
            degree_square = degree * degree
            prior = degree - 1.0
            factor_up = jnp.sqrt(
                jnp.maximum(4.0 * degree_square - 1.0, 1.0)
                / jnp.maximum(degree_square - order_square, 1.0)
            )
            factor_down = jnp.sqrt(
                jnp.maximum(prior * prior - order_square, 0.0)
                / jnp.maximum(4.0 * prior * prior - 1.0, 1.0)
            )
            next_row = factor_up * (cosine * newer_row - factor_down * older_row)
            next_row = jnp.where(
                degree < order_values, 0.0, jnp.where(degree == order_values, diagonal, next_row)
            )
            produced.append(next_row)
            older_row, newer_row = (newer_row, next_row)
        return ((older_row, newer_row), jnp.stack(produced))

    empty = jnp.zeros_like(diagonal)
    carried, stacked = lax.scan(advance, (empty, empty), jnp.arange(turn_count, dtype=jnp.int32))
    return stacked.reshape(turn_count * block_size, orders.shape[0], colatitude.shape[0])[
        :degree_count
    ]


def spectral_values(coefficients, orders):
    degree_count = coefficients.shape[-1]
    degrees = jnp.arange(degree_count, dtype=jnp.int32)
    keep = degrees[None, :] >= orders[:, None]
    factor = math.sqrt(3.0) * math.sqrt(4.0 * math.pi) / degree_count * 2.0 ** (-30)
    values = coefficients.astype(jnp.float32) * factor
    return jnp.where(keep, values, 0.0).astype(jnp.bfloat16)


def fourier_basis(order_count, lon_count):
    orders = jnp.arange(order_count, dtype=jnp.int32)
    columns = jnp.arange(lon_count, dtype=jnp.int32)
    phases = orders[:, None] * columns[None, :] % lon_count
    angles = 2.0 * math.pi / lon_count * phases.astype(jnp.float32)
    weights = jnp.where(orders == 0, 1.0, math.sqrt(2.0)).astype(jnp.float32)[:, None]
    return jnp.stack([weights * jnp.cos(angles), weights * jnp.sin(angles)]).astype(jnp.bfloat16)


def local(weather, coefficients, channel_scale):
    group_count = lax.axis_size("member")
    band_count = lax.axis_size("space")
    member_local, channels, rows_local, lon_count = weather.shape
    order_local = coefficients.shape[3]
    degree_count = coefficients.shape[4]
    order_count = order_local * band_count
    lat_count = rows_local * band_count
    lat_local = rows_local // group_count
    member_count = member_local * group_count
    first_order = lax.axis_index("space") * order_local
    orders = first_order + jnp.arange(order_local, dtype=jnp.int32)
    order_logs = lax.dynamic_slice_in_dim(diagonal_log(order_count), first_order, order_local)
    row_first = (lon_count // 2 + 1 - lat_count) // 2
    colatitude = (
        math.pi
        * (row_first + jnp.arange(lat_count, dtype=jnp.int32)).astype(jnp.float32)
        / (lon_count // 2)
    )
    legendre = legendre_table(orders, colatitude, order_logs, degree_count).astype(jnp.bfloat16)
    spectral = spectral_values(coefficients, orders)
    fourier = jnp.einsum(
        "ecpml,lmt->ectpm", spectral, legendre, preferred_element_type=jnp.float32
    ).astype(jnp.bfloat16)
    fourier = fourier.reshape(
        member_local, channels, band_count, group_count, lat_local, 2, order_local
    )
    basis = fourier_basis(order_count, lon_count).reshape(2 * order_count, lon_count)
    scale_wide = channel_scale[None, :, None, None, None]
    pieces = weather.reshape(member_local, channels, group_count, lat_local, lon_count)
    banded = exchange_both(fourier, ("member", "space"), ("member", "space"), (3, 2), (0, 6))
    fourier_rows = banded.reshape(member_count * channels * lat_local, 2 * order_count)
    noise = jnp.dot(fourier_rows, basis, preferred_element_type=jnp.float32).astype(jnp.bfloat16)
    noise = noise.reshape(member_count, channels, 1, lat_local, lon_count)
    noise_wide = lax.optimization_barrier(noise).astype(jnp.float32)
    band_mean = jnp.sum(noise_wide, axis=0, keepdims=True) / member_count
    weather_bands = lax.all_to_all(pieces, "member", split_axis=2, concat_axis=0, tiled=True)
    perturbed = (weather_bands.astype(jnp.float32) + scale_wide * (noise_wide - band_mean)).astype(
        jnp.bfloat16
    )
    returned = lax.all_to_all(perturbed, "member", split_axis=0, concat_axis=2, tiled=True)
    return returned.reshape(member_local, channels, rows_local, lon_count)


def solution(mesh):
    return jax.shard_map(
        local,
        mesh=mesh,
        in_specs=(P("member", None, "space", None), P("member", None, None, "space", None), P()),
        out_specs=P("member", None, "space", None),
        check_vma=False,
    )
```

profile of v0, /device:TPU:0, one launch (start us, length us, event | category | flops | bytes accessed | tf_op | source)
XLA Modules:
  0.0 521.0 jit_solution(6489075889256272937)
XLA Ops:
  0.9 127.6 %while.21 = (s32[]{:T(128)}, f32[46,256]{1,0:T(8,128)S(1)}, f32[46,256]{1,0:T(8,128)S(1)}, bf16[23,16,46,256]{3,2,1,0:T(8,128)(2,1)}, s32[23]{0:T(128)S(1)}, /*i...) while((s32[]{:T(128)}, f32[46,256]{1,0:T(8,128)S(1)}, ...), condition=%wide.region_3.4_spmd.clone.clone.clone.clone, body=%wide.region_2.3_spmd.clone.clone.clone.clone.sunk | while | flops 3519778 | bytes 3859869 | solution.py:73
  16.7 0.8 bitcast_dynamic-update-slice_fusion.50
  38.8 0.8 bitcast_dynamic-update-slice_fusion.50
  49.9 0.8 bitcast_dynamic-update-slice_fusion.50
  88.7 0.8 bitcast_dynamic-update-slice_fusion.50
  99.8 0.8 bitcast_dynamic-update-slice_fusion.50
  110.9 0.8 bitcast_dynamic-update-slice_fusion.50
  116.5 0.8 bitcast_dynamic-update-slice_fusion.50
  122.1 0.8 bitcast_dynamic-update-slice_fusion.50
  127.7 0.8 bitcast_dynamic-update-slice_fusion.50
  128.5 10.1 %copy.39 = bf16[23,16,46,256]{3,1,0,2:T(8,128)(2,1)} copy(bf16[23,16,46,256]{3,2,1,0:T(8,128)(2,1)} %get-tuple-element.233) | data formatting | bytes 17334272 | tf_op jit(solution)/shard_map/convert.6
  138.6 11.3 %fusion.48 = bf16[84,2,46,361]{3,1,2,0:T(2,128)(2,1)} fusion(s32[1,84,2,46,361]{4,2,3,1,0:T(2,128)} %param.6, pred[46,361]{1,0:T(8,128)(4,1)S(1)} %iota_compare_fusion), kind=kLoop, calls=%fused_computation.136 | loop fusion | flops 11159232 | bytes 16755454 | tf_op jit(solution)/shard_map/reshape.8
  149.9 6.9 %convert_bitcast_fusion = bf16[1,84,256,2,46]{2,1,3,4,0:T(8,128)(2,1)} fusion(bf16[84,2,46,361]{3,1,2,0:T(2,128)(2,1)} %fusion.48, bf16[368,46,256]{2,0,1:T(8,128)(2,1)S(1)} %bitcast.379), kind=kOutput, calls=%fused_computation.137 | convolution fusion | flops 1430360064 | bytes 18203488 | tf_op jit(solution)/shard_map/ecpml,lmt->ectpm/dot_general | solution.py:118
  156.8 7.8 %copy.41 = bf16[1,84,256,2,46]{1,2,4,3,0:T(8,128)(2,1)} copy(bf16[1,84,256,2,46]{2,1,3,4,0:T(8,128)(2,1)} %convert_bitcast_fusion) | data formatting | bytes 7913472 | tf_op jit(solution)/shard_map/convert_element_type | solution.py:120
  164.7 5.7 %copy.55 = bf16[16,8,1,84,1,1,2,2,46]{3,1,0,8,7,6,5,4,2:T(8,128)(2,1)S(1)} copy(bf16[16,8,1,84,1,1,2,2,46]{3,6,0,1,8,7,5,4,2:T(2,128)(2,1)} %bitcast.377) | data formatting | bytes 7913472 | tf_op jit(solution)/shard_map/transpose;transpose | solution.py:24
  170.4 27.3 %copy.43 = bf16[128,1,84,1,1,2,2,46]{2,6,7,5,4,3,1,0:T(2,128)(2,1)} copy(bf16[128,1,84,1,1,2,2,46]{2,0,7,6,5,4,3,1:T(8,128)(2,1)S(1)} %bitcast.378) | data formatting | bytes 7913472 | tf_op jit(solution)/shard_map/reshape | solution.py:26
  197.7 11.7 %all-to-all-start.1 = ((bf16[128,1,84,1,1,2,2,46]{2,6,7,5,4,3,1,0:T(2,128)(2,1)}), bf16[128,1,84,1,1,2,2,46]{2,6,7,5,4,3,1,0:T(2,128)(2,1)}, u32[]{:S(2)}, u32[]{:S(2)}) async-start(bf16[128,1,84,1,1,2,2,46]{2,6,7,5,4,3,1,0:T(2,128)(2,1)} %copy.43), calls=%async_computation.1 | async-start | bytes 12058624 | tf_op jit(solution)/shard_map/all_to_all | solution.py:27
  209.3 11.3 %copy.36 = bf16[1,84,32,1440]{3,1,2,0:T(8,128)(2,1)} copy(bf16[1,84,32,1440]{3,2,1,0:T(8,128)(2,1)} %param.5) | data formatting | bytes 15482880 | tf_op args[0]
  220.7 12.9 %copy.37 = bf16[1,84,16,2,1440]{4,3,1,0,2:T(2,128)(2,1)} copy(bf16[1,84,16,2,1440]{4,1,3,2,0:T(8,128)(2,1)} %bitcast.375) | data formatting | bytes 15482880 | tf_op jit(solution)/shard_map/reshape | solution.py:126
  233.6 49.0 %all-to-all-done.1 = bf16[128,1,84,1,1,2,2,46]{2,6,7,5,4,3,1,0:T(2,128)(2,1)} async-done(((bf16[128,1,84,1,1,2,2,46]{2,6,7,5,4,3,1,0:T(2,128)(2,1)}), bf16[128,1,84,1,1,2,2,46]{2,6,7,5,4,3,1,0:T(2,128)(2,1)}, u32[]{:S(2)}, u32[]{:S(2)}) %all-to-all-start.1) | async-done | bytes 3956768 | tf_op jit(solution)/shard_map/all_to_all | solution.py:27
  282.6 4.9 all-to-all-start
  287.5 9.8 %multiply_convert_fusion.1 = (bf16[1,368,1440]{2,1,0:T(8,128)(2,1)S(1)}, bf16[1,368,1440]{2,1,0:T(8,128)(2,1)S(1)}) fusion(f32[368]{0:T(512)S(1)} %fusion.58), kind=kLoop, calls=%fused_computation.143 | loop fusion | flops 6888960 | bytes 2121152 | tf_op jit(solution)/shard_map/convert.3
  297.5 24.1 %copy.44 = bf16[16,8,1,84,1,1,2,2,46]{8,1,7,6,3,0,5,4,2:T(8,128)(2,1)} copy(bf16[16,8,1,84,1,1,2,2,46]{3,7,8,6,1,0,5,4,2:T(2,128)(2,1)} %bitcast.18) | data formatting | bytes 7913472 | tf_op jit(solution)/shard_map/reshape | solution.py:28
  321.7 16.2 %reshape_reshape.7 = bf16[2688,736]{1,0:T(8,128)(2,1)} reshape(bf16[16,84,1,1,2,2,8,46]{7,6,5,4,1,0,3,2:T(8,128)(2,1)} %bitcast.373) | data formatting | bytes 7913472 | tf_op jit(solution)/shard_map/reshape;reshape | solution.py:128
  337.8 11.2 %convolution_convert_fusion = bf16[2688,1440]{0,1:T(8,128)(2,1)} fusion(bf16[2688,736]{1,0:T(8,128)(2,1)} %reshape_reshape.7, bf16[736,1440]{1,0:T(8,128)(2,1)S(1)} %bitcast.396), kind=kOutput, calls=%fused_computation.130 | convolution fusion | flops 5701570560 | bytes 13817856 | tf_op jit(solution)/shard_map/dot_general | solution.py:129
  349.0 11.6 %copy.45 = bf16[2688,1440]{1,0:T(8,128)(2,1)} copy(bf16[2688,1440]{0,1:T(8,128)(2,1)} %convolution_convert_fusion) | data formatting | bytes 15482880 | tf_op jit(solution)/shard_map/convert_element_type | solution.py:129
  360.6 17.0 %reshape.1212 = bf16[16,84,1,2,1440]{4,3,1,0,2:T(2,128)(2,1)} reshape(bf16[2688,1440]{1,0:T(8,128)(2,1)} %copy.45) | data formatting | bytes 15482880 | tf_op jit(solution)/shard_map/reshape | solution.py:130
  377.6 9.6 %convert_reduce_fusion = f32[84,2,1440]{2,1,0:T(2,128)S(1)} fusion(bf16[16,84,1,2,1440]{4,3,1,0,2:T(2,128)(2,1)} %reshape.1212), kind=kLoop, calls=%fused_computation.125 | loop fusion | flops 7499520 | bytes 8709120 | tf_op jit(solution)/shard_map/reduce_sum | solution.py:132
  387.7 15.5 %fusion.46 = bf16[16,84,1,2,1440]{4,3,2,1,0:T(2,128)(2,1)S(1)} fusion(f32[84,2,1440]{2,1,0:T(2,128)S(1)} %broadcast_multiply_fusion, bf16[16,84,1,2,1440]{4,3,1,0,2:T(2,128)(2,1)} %reshape.1212, f32[84]{0:T(128)S(1)} %copy-done.1, bf16[1,84,16,2,1440]{4,3,1,0,2:T(2,128)(2,1)} %all-to-all-done), kind=kLoop, calls=%fused_computation.133 | loop fusion | flops 23224320 | bytes 24192336 | tf_op jit(solution)/shard_map/convert_element_type | solution.py:134
  403.2 99.3 %all_to_all.29 = bf16[16,84,1,2,1440]{4,3,2,1,0:T(2,128)(2,1)} all-to-all(bf16[16,84,1,2,1440]{4,3,2,1,0:T(2,128)(2,1)S(1)} %fusion.46), channel_id=1, replica_groups=mesh['member'=16,'space'=8] {'member'}, dimensions={0} | all-to-all | bytes 15482880 | tf_op jit(solution)/shard_map/all_to_all | solution.py:137
  502.6 8.5 %copy.47 = bf16[1,84,16,1,2,1440]{5,1,4,2,3,0:T(8,128)(2,1)} copy(bf16[1,84,16,1,2,1440]{5,4,1,2,3,0:T(2,128)(2,1)} %bitcast.376) | data formatting | bytes 15482880 | tf_op jit(solution)/shard_map/all_to_all | solution.py:137
  511.0 9.5 %copy.48 = bf16[1,84,32,1440]{3,2,1,0:T(8,128)(2,1)} copy(bf16[1,84,32,1440]{3,1,2,0:T(8,128)(2,1)} %bitcast.374) | data formatting | bytes 15482880 | tf_op jit(solution)/shard_map/reshape | solution.py:138
  (1188 shorter events, 94.9 us)
Async XLA Ops:
  138.6 11.3 %copy-start = (bf16[23,16,46,256]{3,1,0,2:T(8,128)(2,1)S(1)}, bf16[23,16,46,256]{3,1,0,2:T(8,128)(2,1)}, u32[]{:S(2)}) copy-start(bf16[23,16,46,256]{3,1,0,2:T(8,128)(2,1)} %copy.39) | copy-start | bytes 26001412
  197.7 84.9 %all-to-all-start.1 = ((bf16[128,1,84,1,1,2,2,46]{2,6,7,5,4,3,1,0:T(2,128)(2,1)}), bf16[128,1,84,1,1,2,2,46]{2,6,7,5,4,3,1,0:T(2,128)(2,1)}, u32[]{:S(2)}, u32[]{:S(2)}) async-start(bf16[128,1,84,1,1,2,2,46]{2,6,7,5,4,3,1,0:T(2,128)(2,1)} %copy.43), calls=%async_computation.1 | async-start | bytes 12058624 | tf_op jit(solution)/shard_map/all_to_all | solution.py:27
  282.6 105.1 %all-to-all-start = ((bf16[1,84,16,2,1440]{4,3,1,0,2:T(2,128)(2,1)}), bf16[1,84,16,2,1440]{4,3,1,0,2:T(2,128)(2,1)}, u32[]{:S(2)}, u32[]{:S(2)}) async-start(bf16[1,84,16,2,1440]{4,3,1,0,2:T(2,128)(2,1)} %copy.37), calls=%async_computation | async-start | bytes 16515072 | tf_op jit(solution)/shard_map/all_to_all | solution.py:133
  377.6 10.1 %copy-start.1 = (f32[84]{0:T(128)S(1)}, f32[84]{0:T(128)}, u32[]{:S(2)}) copy-start(f32[84]{0:T(128)} %param.7) | copy-start | bytes 1012
where the time goes:
time: 530 us; the launch traced here: 521 us
  local copies, waits for them, and re-layouts  195 us (37%)
  other arithmetic  115 us (22%)
  blocking collectives  99.3 us (19%)
  waiting for transfers between devices  49 us (9%)
  loops' own time  27.1 us (5%)
  matrix products  18.1 us (3%)
  starting transfers between devices  16.6 us (3%)
    all_to_all x1, blocking collectives, local(): lax.all_to_all(perturbed, 'member', split_axis=0, concat_axis=2, tiled=True)  99.3 us
    while x345, other arithmetic  53.9 us
    all_to_all x1, waiting for transfers between devices, exchange_both(): parts = lax.all_to_all(parts, axis, split_axis=0, concat_axis=0, tiled=True)  49 us
    reshape x1, local copies, waits for them, and re-layouts, exchange_both(): parts = parts.reshape(-1, *inside)  27.3 us
    another operation x1, loops' own time, legendre_table(): lax.scan(advance, (empty, empty), jnp.arange(turn_count, dtype=jnp.int32))  27.1 us
    reshape x1, local copies, waits for them, and re-layouts, exchange_both(): parts = joined_along(parts.reshape(*sizes, *inside), concats[0] + 1)  24.1 us
    another operation x5, other arithmetic  21.5 us
    dynamic_update_slice x23, local copies, waits for them, and re-layouts, legendre_table(): lax.scan(advance, (empty, empty), jnp.arange(turn_count, dtype=jnp.int32))  18.2 us
  transfers between devices with their start and end apart: 2, of which 1 were waited for; matrix products, arithmetic and copies ran while one was open for 24% of the time, Pallas kernels for 0%

commit v1 on v0

v1 whole, which is shorter than its diff:
```python
import functools
import math

import jax
import jax.numpy as jnp
import numpy as np
from jax import lax
from jax.experimental import pallas as pl
from jax.experimental.pallas import tpu as pltpu
from jax.sharding import PartitionSpec as P

MESH = pl.DeviceIdType.MESH
F32 = jnp.float32
BF16 = jnp.bfloat16
CB = 12
GR = CB // 4
LPAD = 384


def seeds(order_local, shards, lat, lat0, lon):
    rows = order_local + 2
    m_all = np.arange(shards * order_local + 8, dtype=np.float64)
    steps = np.maximum(m_all, 1.0)
    terms = np.where(m_all > 0, 0.5 * np.log((2.0 * steps + 1.0) / (2.0 * steps)), 0.0)
    logs = np.cumsum(terms) - 0.5 * math.log(4.0 * math.pi)
    index = order_local * np.arange(shards)[:, None] + np.arange(rows)[None, :]
    diag = np.broadcast_to(logs[index].reshape(-1, 1), (shards * rows, 128))
    colat = math.pi * (lat0 + np.arange(lat)) / (lon // 2)
    angle = np.broadcast_to(
        np.stack([np.cos(colat), np.log(np.sin(colat))])[:, None, :], (2, 8, lat)
    )
    degree = np.arange(LPAD, dtype=np.float64)
    factors = np.stack(
        [
            np.sqrt(np.maximum(4.0 * degree**2 - 1.0, 1.0)),
            1.0 / np.sqrt(np.maximum(4.0 * (degree - 1.0) ** 2 - 1.0, 1.0)),
        ]
    )
    lane = np.arange(1536)
    theta = np.where(lane < lon, 2.0 * math.pi * lane / lon, 0.0)[None, :]
    m = (np.arange(8) // 2)[:, None]
    p = (np.arange(8) % 2)[:, None]
    turn = []
    for by in (4, order_local):
        turn += [np.broadcast_to(f(by * theta), (8, 1536)) for f in (np.cos, np.sin)]
    wave = np.stack([np.cos(m * theta - p * math.pi / 2), np.sin(m * theta - p * math.pi / 2)] + turn)
    return [np.asarray(a, np.float32) for a in (diag, angle, factors, wave)]


def kernel(
    dims, weather, coefs, scale, diag, angle, factors, wave, out,
    cbuf, stage, table, four, held, hsend, hrecv, zsend, zrecv, xsend, xrecv,
    msend, mrecv, aown, apar, got, rows, basis, field,
    csem, wsem, osem, hs, hr, zs, zr, xs, xr, ms, mr, sown, spar, ar,
):
    chunks, order_local, degrees, lat, lon, shards, factor = dims
    half = shards // 2
    me = lax.axis_index("member")
    sp = lax.axis_index("space")
    core = lax.rem(me, 2)
    other = me + 1 - 2 * core
    across = me + 2 - 4 * lax.rem(me // 2, 2)
    zpos = me // 4
    ring = [lax.rem(zpos + j, 4) * 4 + lax.rem(me, 4) for j in range(4)]
    mine = core * half
    theirs = (1 - core) * half

    barrier = pltpu.get_barrier_semaphore()
    for j in range(1, 4):
        pl.semaphore_signal(barrier, inc=1, device_id=(ring[j], sp), device_id_type=MESH)
    pl.semaphore_signal(barrier, inc=1, device_id=(across, sp), device_id_type=MESH)
    pl.semaphore_signal(barrier, inc=1, device_id=(other, sp), device_id_type=MESH)
    for j in range(1, shards):
        there = lax.rem(sp + j, shards)
        pl.semaphore_signal(barrier, inc=1, device_id=(me, there), device_id_type=MESH)
        pl.semaphore_signal(barrier, inc=1, device_id=(other, there), device_id_type=MESH)

    def coef_copy(n):
        slot = lax.rem(n, 2)
        return pltpu.make_async_copy(coefs.at[0, pl.ds(n * CB, CB)], cbuf.at[slot], csem.at[slot])

    def weather_copy(n):
        return pltpu.make_async_copy(
            weather.at[0, pl.ds(n * CB, CB)], field.at[pl.ds(n * CB, CB)], wsem.at[n]
        )

    def out_copy(n):
        return pltpu.make_async_copy(
            field.at[pl.ds(n * CB, CB)], out.at[0, pl.ds(n * CB, CB)], osem.at[n]
        )

    coef_copy(0).start()
    coef_copy(1).start()
    for n in range(chunks):
        weather_copy(n).start()

    four[...] = jnp.zeros_like(four)
    nrow = order_local + 2
    m_row = (lax.broadcasted_iota(jnp.int32, (nrow, 128), 0) + sp * order_local).astype(F32)
    m_sq = m_row * m_row
    m_wide = jnp.concatenate([m_row, m_row], axis=1)
    cosine = jnp.broadcast_to(angle[0, 0:1, :], (nrow, lat))
    lsine = jnp.broadcast_to(angle[1, 0:1, :], (nrow, lat))
    dlog = diag[pl.ds(pl.multiple_of(sp * nrow, 8), nrow), :]
    first = jnp.exp(jnp.concatenate([dlog, dlog], axis=1) + m_wide * lsine)

    def block(b, carry):
        older, newer, q = carry
        for i in range(16):
            l = b * 16 + i
            lf = l.astype(F32)
            gap = lf * lf - m_sq
            r = lax.rsqrt(jnp.maximum(gap, 1.0))
            up = factors[0, l] * r
            down = factors[1, l] * q
            up2 = jnp.concatenate([up, up], axis=1)
            down2 = jnp.concatenate([down, down], axis=1)
            nxt = up2 * (cosine * newer - down2 * older)
            nxt = jnp.where(m_wide == lf, first, nxt)
            q = jnp.maximum(gap, 0.0) * r
            older, newer = newer, nxt
            for v in range(lat // 128):
                stage[v, pl.ds(i, nrow, stride=17), :] = nxt[:, 128 * v : 128 * v + 128]

        def put(m, c):
            for v in range(lat // 128):
                table[m, pl.ds(pl.multiple_of(b * 16, 16), 16), 128 * v : 128 * v + 128] = stage[
                    v, pl.ds(m * 17, 16), :
                ].astype(BF16)
            return c

        lax.fori_loop(0, order_local, put, 0, unroll=2)
        return older, newer, q

    empty = jnp.zeros((nrow, lat), F32)
    blocks = (degrees + 15) // 16
    lax.fori_loop(0, blocks, block, (empty, empty, jnp.zeros((nrow, 128), F32)))
    for m in range(order_local):
        if blocks * 16 < LPAD:
            table[m, blocks * 16 :, :] = jnp.zeros((LPAD - blocks * 16, lat), BF16)

    pl.semaphore_wait(barrier, 2 * (shards - 1) + 5)

    def make_basis():
        turn = [wave[2 + i] for i in range(4)]
        root2 = math.sqrt(2.0)

        def shard_rows(s, carry):
            u0, v0 = carry
            u, v = u0, v0
            for b in range(12):
                w = jnp.full((8, 1536), root2, F32)
                row = lax.broadcasted_iota(jnp.int32, (8, 1536), 0) + b * 8
                if b == 0:
                    w = jnp.where((row < 2) & (s == 0), 1.0, w)
                if b == 11:
                    w = jnp.where(row < 2 * order_local, w, 0.0)
                wide[pl.ds(b * 8, 8), :] = w * u
                u, v = u * turn[0] - v * turn[1], v * turn[0] + u * turn[1]
            basis[pl.ds(pl.multiple_of(s * 96, 16), 96), :] = wide[...].astype(BF16)
            return u0 * turn[2] - v0 * turn[3], v0 * turn[2] + u0 * turn[3]

        lax.fori_loop(0, shards, shard_rows, (wave[0], wave[1]))

    wide = rows
    make_basis()

    lane = lax.broadcasted_iota(jnp.int32, (8, 128), 1) // 32
    sub = lax.broadcasted_iota(jnp.int32, (8, 128), 0) // 2
    shift = lax.rem(lane - sub + 4, 4)
    masks = [shift == d for d in range(4)]
    degree_i = lax.broadcasted_iota(jnp.int32, (2 * CB, degrees), 1)

    def pair_copy(n):
        return pltpu.make_async_remote_copy(
            hsend.at[n], hrecv.at[n], hs.at[n], hr.at[n], device_id=(other, sp), device_id_type=MESH
        )

    def ring_copy(n, j):
        return pltpu.make_async_remote_copy(
            zsend.at[n, lax.rem(zpos + j, 4)], zrecv.at[n, j - 1], zs.at[n, j - 1], zr.at[n, j - 1],
            device_id=(ring[j], sp), device_id_type=MESH,
        )

    def across_copy(n):
        return pltpu.make_async_remote_copy(
            xsend.at[n], xrecv.at[n], xs.at[n], xr.at[n], device_id=(across, sp), device_id_type=MESH
        )

    def mean_copy(n, j):
        return pltpu.make_async_remote_copy(
            msend.at[n], mrecv.at[n, j - 1], ms.at[n, j - 1], mr.at[n, j - 1],
            device_id=(ring[j], sp), device_id_type=MESH,
        )

    def own_copy(n, i):
        return pltpu.make_async_remote_copy(
            aown.at[n, i], got.at[n, sp], sown.at[n, i], ar.at[n, sp],
            device_id=(me, mine + i), device_id_type=MESH,
        )

    def partner_copy(n, i):
        return pltpu.make_async_remote_copy(
            apar.at[n, i], got.at[n, sp], spar.at[n, i], ar.at[n, sp],
            device_id=(other, mine + i), device_id_type=MESH,
        )

    def arrival(n, s):
        return pltpu.make_async_remote_copy(
            aown.at[n, 0], got.at[n, s], sown.at[n, 0], ar.at[n, s],
            device_id=(other, sp), device_id_type=MESH,
        )

    def legendre(n):
        slot = lax.rem(n, 2)
        coef_copy(n).wait()

        def order(h, c):
            for e in range(2):
                m = h * 2 + e
                values = cbuf[slot, :, m].reshape(2 * CB, degrees).astype(F32) * factor
                lhs = jnp.where(degree_i >= sp * order_local + m, values, 0.0).astype(BF16)
                res = jnp.dot(lhs, table[m, 0:degrees, :], preferred_element_type=F32)
                for g in range(GR):
                    for v in range(lat // 128):
                        part = res[8 * g : 8 * g + 8, 128 * v : 128 * v + 128]
                        turned = part
                        for d in range(1, 4):
                            moved = pltpu.roll(pltpu.roll(part, 8 - 2 * d, 0), 32 * d, 1)
                            turned = jnp.where(masks[d], moved, turned)
                        for dd in range(4):
                            four[v * 4 + dd, g, pl.ds(h * 4 + 2 * e, 2), :] = turned[2 * dd : 2 * dd + 2, :]
            return c

        lax.fori_loop(0, order_local // 2, order, 0)
        @pl.when(n + 2 < chunks)
        def _():
            coef_copy(n + 2).start()

        for i in range(half):
            held[n, i] = four[mine + i].astype(BF16)
            hsend[n, i] = four[theirs + i].astype(BF16)
        pair_copy(n).start()

    def start_ring(n):
        pair_copy(n).wait_recv()
        for i in range(half):
            zsend[n, i] = (held[n, i].astype(F32) + hrecv[n, i].astype(F32)).astype(BF16)
        for j in (2, 1, 3):
            ring_copy(n, j).start()

    def start_across(n):
        total = zsend[n, zpos].astype(F32)
        for j in range(1, 4):
            ring_copy(n, j).wait_recv()
            total = total + zrecv[n, j - 1].astype(F32)
        xsend[n] = total.astype(BF16)
        across_copy(n).start()

    def start_mean(n):
        across_copy(n).wait_recv()
        total = xsend[n].astype(F32) + xrecv[n].astype(F32)
        msend[n] = (total * (1.0 / 16.0)).astype(BF16)
        for j in (2, 1, 3):
            mean_copy(n, j).start()

    def start_exchange(n):
        for j in range(4):
            i = lax.rem(zpos - j + 4, 4)
            if j == 0:
                mean = msend[n].astype(F32)
            else:
                mean_copy(n, j).wait_recv()
                mean = mrecv[n, j - 1].astype(F32)
            aown[n, i] = (held[n, i].astype(F32) - mean).astype(BF16)
            apar[n, i] = (hrecv[n, i].astype(F32) - mean).astype(BF16)
        for j in range(4):
            i = lax.rem(sp + 2 + j, 4)
            partner_copy(n, i).start()

            @pl.when(mine + i != sp)
            def _():
                own_copy(n, i).start()

            @pl.when(mine + i == sp)
            def _():
                got[n, sp] = aown[n, i]

    def finish(n):
        for s in range(shards):
            @pl.when(jnp.logical_or(s != sp, sp // half != core))
            def _():
                arrival(n, s).wait_recv()

        weather_copy(n).wait()
        lhs = []
        for g in range(GR):
            lhs.append(got[n, :, g].reshape(shards * 96, 128).T)
        lhs = jnp.concatenate(lhs, axis=0)
        for b in range(6):
            lo = b * 256
            width = min(256, lon - lo)
            res = jnp.dot(lhs, basis[:, lo : lo + 256], preferred_element_type=F32)
            for c in range(CB):
                k = n * CB + c
                old = field[k, :, lo : lo + width].astype(F32)
                field[k, :, lo : lo + width] = (
                    old + scale[k] * res[32 * c : 32 * c + 32, :width]
                ).astype(BF16)
        out_copy(n).start()

    def tick(n, carry):
        def stage_at(lag, f):
            @pl.when(jnp.logical_and(n >= lag, n < chunks + lag))
            def _():
                f(n - lag)

        stage_at(0, legendre)
        stage_at(1, start_across)
        stage_at(2, start_mean)
        stage_at(3, start_exchange)
        stage_at(0, start_ring)
        stage_at(4, finish)
        return carry

    lax.fori_loop(0, chunks + 4, tick, 0)

    def drain(n, carry):
        out_copy(n).wait()
        pair_copy(n).wait_send()
        across_copy(n).wait_send()
        for j in range(1, 4):
            ring_copy(n, j).wait_send()
            mean_copy(n, j).wait_send()
        for i in range(half):
            partner_copy(n, i).wait_send()

            @pl.when(mine + i != sp)
            def _():
                own_copy(n, i).wait_send()

        return carry

    lax.fori_loop(0, chunks, drain, 0)


def local(weather, coefficients, channel_scale):
    shards = lax.axis_size("space")
    _, channels, rows_local, lon = weather.shape
    order_local, degrees = coefficients.shape[3:]
    lat = rows_local * shards
    lat0 = (lon // 2 + 1 - lat) // 2
    chunks = channels // CB
    half = shards // 2
    factor = math.sqrt(3.0) * math.sqrt(4.0 * math.pi) / degrees * 2.0 ** (-30)
    diag, angle, factors, wave = seeds(order_local, shards, lat, lat0, lon)
    piece = (GR, 96, 128)
    V = pltpu.VMEM
    D = pltpu.SemaphoreType.DMA
    any_ = pl.BlockSpec(memory_space=pl.ANY)
    vmem = pl.BlockSpec(memory_space=pltpu.VMEM)
    smem = pl.BlockSpec(memory_space=pltpu.SMEM)
    dims = (chunks, order_local, degrees, lat, lon, shards, factor)
    return pl.pallas_call(
        functools.partial(kernel, dims),
        out_shape=jax.ShapeDtypeStruct(weather.shape, weather.dtype),
        in_specs=[any_, any_, smem, vmem, vmem, smem, vmem],
        out_specs=any_,
        scratch_shapes=[
            V((2, CB, order_local, 2, degrees), jnp.int32),
            V((lat // 128, (order_local + 2) * 17, 128), F32),
            V((order_local, LPAD, lat), BF16),
            V((shards,) + piece, F32),
            V((chunks, half) + piece, BF16),
            V((chunks, half) + piece, BF16),
            V((chunks, half) + piece, BF16),
            V((chunks, 4) + piece, BF16),
            V((chunks, 3) + piece, BF16),
            V((chunks,) + piece, BF16),
            V((chunks,) + piece, BF16),
            V((chunks,) + piece, BF16),
            V((chunks, 3) + piece, BF16),
            V((chunks, half) + piece, BF16),
            V((chunks, half) + piece, BF16),
            V((chunks, shards) + piece, BF16),
            V((96, 1536), F32),
            V((shards * 96, 1536), BF16),
            V((channels, rows_local, lon), BF16),
            D((2,)), D((chunks,)), D((chunks,)),
            D((chunks,)), D((chunks,)),
            D((chunks, 3)), D((chunks, 3)),
            D((chunks,)), D((chunks,)),
            D((chunks, 3)), D((chunks, 3)),
            D((chunks, half)), D((chunks, half)), D((chunks, shards)),
        ],
        compiler_params=pltpu.CompilerParams(
            collective_id=0, has_side_effects=True, vmem_limit_bytes=67043328
        ),
        name="synthesis",
    )(weather, coefficients.transpose(0, 1, 3, 2, 4), channel_scale, diag, angle, factors, wave)


def solution(mesh):
    return jax.shard_map(
        local,
        mesh=mesh,
        in_specs=(P("member", None, "space", None), P("member", None, None, "space", None), P()),
        out_specs=P("member", None, "space", None),
        check_vma=False,
    )
```

time: 530 us -> 120 us (0.23); the launches traced: 521 us -> 120 us
  local copies, waits for them, and re-layouts: 195 us -> 7.72 us
  other arithmetic: 115 us -> 0 us
  Pallas kernels: 0 us -> 112 us
  blocking collectives: 99.3 us -> 0 us
  waiting for transfers between devices: 49 us -> 0 us
  loops' own time: 27.1 us -> 0 us
  matrix products: 18.1 us -> 0 us
  starting transfers between devices: 16.6 us -> 0 us
    pallas_call x0 -> x1, Pallas kernels: none -> 112 us  [local(): pl.pallas_call(functools.partial(kernel, dims), out_shape=jax.ShapeDtypeS...]
    all_to_all x1 -> x0, blocking collectives: 99.3 us -> none  [local(): lax.all_to_all(perturbed, 'member', split_axis=0, concat_axis=2, tiled=True)]
    reshape x6 -> x0, local copies, waits for them, and re-layouts: 90.9 us -> none  [the longest x1 27.3 us: exchange_both(): parts = parts.reshape(-1, *inside)]
    while x345 -> x0, other arithmetic: 53.9 us -> none
    all_to_all x2 -> x0, waiting for transfers between devices: 49 us -> none  [the longest x1 49 us: exchange_both(): parts = lax.all_to_all(parts, axis, split_axis=0, concat_axis=0, tiled=True)]
    another operation x4 -> x0, local copies, waits for them, and re-layouts: 32.1 us -> none  [the longest x1 16.2 us: local(): banded.reshape(member_count * channels * lat_local, 2 * order_count)]
    another operation x1 -> x0, loops' own time: 27.1 us -> none  [legendre_table(): lax.scan(advance, (empty, empty), jnp.arange(turn_count, dtype=jnp.int32))]
    another operation x29 -> x0, other arithmetic: 24.8 us -> none
  transfers between devices with their start and end apart: 2 -> 0, of which waited for: 1 -> 0; matrix products, arithmetic and copies ran while one was open for 24% -> 0% of each run, Pallas kernels for 0% -> 0%
where the time goes in v1:
time: 120 us
  Pallas kernels  112 us (93%)
  local copies, waits for them, and re-layouts  7.72 us (6%)
    pallas_call x1, Pallas kernels, local(): pl.pallas_call(functools.partial(kernel, dims), out_shape=jax.ShapeDtypeS...  112 us
    unnamed x1, local copies, waits for them, and re-layouts  7.72 us

profile of v1, /device:TPU:0, one launch (start us, length us, event | category | flops | bytes accessed | tf_op | source)
XLA Modules:
  0.0 119.9 jit_solution(9895580346073093941)
XLA Ops:
  0.0 112.2 %synthesis.1 = bf16[1,84,32,1440]{3,2,1,0:T(8,128)(2,1)} custom-call(bf16[1,84,32,1440]{3,2,1,0:T(8,128)(2,1)} %weather.1, s32[1,84,46,2,361]{4,3,2,1,0:T(2,128)} %bitcast.1, f32[84]{0:T(128)} %scale.1, f32[384,128]{1,0:T(8,128)} %constant.8.clone.diag, f32[2,8,256]{2,1,0:T(8,128)} %constant.9.clone.angle, f32[2,384]{1,0:T(2,128)} %constant.10.clone.factors, ...), custom_call_target="tpu_custom_call" | custom-call | tf_op jit(solution)/shard_map/synthesis/pallas_call | solution.py:364
  112.2 7.7 %copy.9 = bf16[1,84,32,1440]{3,2,1,0:T(8,128)(2,1)} copy(bf16[1,84,32,1440]{3,2,1,0:T(8,128)(2,1)} %synthesis.1) | data formatting | bytes 15482880

commit v2 on v1

--- a/solution.py
+++ b/solution.py
@@ -15,6 +15,7 @@
 CB = 12
 GR = CB // 4
 LPAD = 384
+UNROLL = 23
 
 
 def seeds(order_local, shards, lat, lat0, lon):
@@ -44,14 +45,21 @@
     for by in (4, order_local):
         turn += [np.broadcast_to(f(by * theta), (8, 1536)) for f in (np.cos, np.sin)]
     wave = np.stack([np.cos(m * theta - p * math.pi / 2), np.sin(m * theta - p * math.pi / 2)] + turn)
-    return [np.asarray(a, np.float32) for a in (diag, angle, factors, wave)]
+    diag = diag.reshape(shards, rows, 128).transpose(1, 0, 2).reshape(rows, -1)
+    lanes = np.repeat(factors.reshape(2, -1, 32).transpose(0, 2, 1), 128, axis=2).reshape(64, -1)
+    tables = np.zeros((64 + rows + 64, 1536))
+    tables[:48] = wave.reshape(48, 1536)
+    tables[48:64, :lat] = angle.reshape(16, lat)
+    tables[64 : 64 + rows, : diag.shape[1]] = diag
+    tables[64 + rows :] = lanes
+    return np.asarray(tables, np.float32)
 
 
 def kernel(
-    dims, weather, coefs, scale, diag, angle, factors, wave, out,
+    dims, weather, coefs, scale, tables, out,
     cbuf, stage, table, four, held, hsend, hrecv, zsend, zrecv, xsend, xrecv,
-    msend, mrecv, aown, apar, got, rows, basis, field,
-    csem, wsem, osem, hs, hr, zs, zr, xs, xr, ms, mr, sown, spar, ar,
+    msend, mrecv, aown, apar, got, rows, basis,
+    csem, wsem, hs, hr, zs, zr, xs, xr, ms, mr, sown, spar, ar,
 ):
     chunks, order_local, degrees, lat, lon, shards, factor = dims
     half = shards // 2
@@ -62,8 +70,10 @@
     across = me + 2 - 4 * lax.rem(me // 2, 2)
     zpos = me // 4
     ring = [lax.rem(zpos + j, 4) * 4 + lax.rem(me, 4) for j in range(4)]
-    mine = core * half
-    theirs = (1 - core) * half
+    def band(c, i):
+        return lax.rem(c + i // 2, 2) * half + i
+
+    mine_is = lax.rem(sp // half + lax.rem(sp, half) // 2, 2) == core
 
     barrier = pltpu.get_barrier_semaphore()
     for j in range(1, 4):
@@ -81,12 +91,7 @@
 
     def weather_copy(n):
         return pltpu.make_async_copy(
-            weather.at[0, pl.ds(n * CB, CB)], field.at[pl.ds(n * CB, CB)], wsem.at[n]
-        )
-
-    def out_copy(n):
-        return pltpu.make_async_copy(
-            field.at[pl.ds(n * CB, CB)], out.at[0, pl.ds(n * CB, CB)], osem.at[n]
+            weather.at[0, pl.ds(n * CB, CB)], out.at[0, pl.ds(n * CB, CB)], wsem.at[n]
         )
 
     coef_copy(0).start()
@@ -99,20 +104,24 @@
     m_row = (lax.broadcasted_iota(jnp.int32, (nrow, 128), 0) + sp * order_local).astype(F32)
     m_sq = m_row * m_row
     m_wide = jnp.concatenate([m_row, m_row], axis=1)
-    cosine = jnp.broadcast_to(angle[0, 0:1, :], (nrow, lat))
-    lsine = jnp.broadcast_to(angle[1, 0:1, :], (nrow, lat))
-    dlog = diag[pl.ds(pl.multiple_of(sp * nrow, 8), nrow), :]
+    cosine = jnp.broadcast_to(tables[48:49, 0:lat], (nrow, lat))
+    lsine = jnp.broadcast_to(tables[56:57, 0:lat], (nrow, lat))
+    dlog = tables[64 : 64 + nrow, pl.ds(pl.multiple_of(sp * 128, 128), 128)]
     first = jnp.exp(jnp.concatenate([dlog, dlog], axis=1) + m_wide * lsine)
 
     def block(b, carry):
         older, newer, q = carry
+        spot = pl.ds(pl.multiple_of(b // 2 * 128, 128), 128)
+        line = 64 + nrow + lax.rem(b, 2) * 16
+        ups = tables[pl.ds(pl.multiple_of(line, 8), 16), spot]
+        downs = tables[pl.ds(pl.multiple_of(line + 32, 8), 16), spot]
         for i in range(16):
             l = b * 16 + i
             lf = l.astype(F32)
             gap = lf * lf - m_sq
             r = lax.rsqrt(jnp.maximum(gap, 1.0))
-            up = factors[0, l] * r
-            down = factors[1, l] * q
+            up = ups[i : i + 1, :] * r
+            down = downs[i : i + 1, :] * q
             up2 = jnp.concatenate([up, up], axis=1)
             down2 = jnp.concatenate([down, down], axis=1)
             nxt = up2 * (cosine * newer - down2 * older)
@@ -142,7 +151,7 @@
     pl.semaphore_wait(barrier, 2 * (shards - 1) + 5)
 
     def make_basis():
-        turn = [wave[2 + i] for i in range(4)]
+        turn = [tables[16 + 8 * i : 24 + 8 * i, :] for i in range(4)]
         root2 = math.sqrt(2.0)
 
         def shard_rows(s, carry):
@@ -160,10 +169,9 @@
             basis[pl.ds(pl.multiple_of(s * 96, 16), 96), :] = wide[...].astype(BF16)
             return u0 * turn[2] - v0 * turn[3], v0 * turn[2] + u0 * turn[3]
 
-        lax.fori_loop(0, shards, shard_rows, (wave[0], wave[1]))
+        lax.fori_loop(0, shards, shard_rows, (tables[0:8, :], tables[8:16, :]))
 
     wide = rows
-    make_basis()
 
     lane = lax.broadcasted_iota(jnp.int32, (8, 128), 1) // 32
     sub = lax.broadcasted_iota(jnp.int32, (8, 128), 0) // 2
@@ -196,13 +204,13 @@
     def own_copy(n, i):
         return pltpu.make_async_remote_copy(
             aown.at[n, i], got.at[n, sp], sown.at[n, i], ar.at[n, sp],
-            device_id=(me, mine + i), device_id_type=MESH,
+            device_id=(me, band(core, i)), device_id_type=MESH,
         )
 
     def partner_copy(n, i):
         return pltpu.make_async_remote_copy(
             apar.at[n, i], got.at[n, sp], spar.at[n, i], ar.at[n, sp],
-            device_id=(other, mine + i), device_id_type=MESH,
+            device_id=(other, band(core, i)), device_id_type=MESH,
         )
 
     def arrival(n, s):
@@ -216,8 +224,8 @@
         coef_copy(n).wait()
 
         def order(h, c):
-            for e in range(2):
-                m = h * 2 + e
+            for e in range(UNROLL):
+                m = h * UNROLL + e
                 values = cbuf[slot, :, m].reshape(2 * CB, degrees).astype(F32) * factor
                 lhs = jnp.where(degree_i >= sp * order_local + m, values, 0.0).astype(BF16)
                 res = jnp.dot(lhs, table[m, 0:degrees, :], preferred_element_type=F32)
@@ -229,17 +237,17 @@
                             moved = pltpu.roll(pltpu.roll(part, 8 - 2 * d, 0), 32 * d, 1)
                             turned = jnp.where(masks[d], moved, turned)
                         for dd in range(4):
-                            four[v * 4 + dd, g, pl.ds(h * 4 + 2 * e, 2), :] = turned[2 * dd : 2 * dd + 2, :]
+                            four[v * 4 + dd, g, pl.ds(2 * m, 2), :] = turned[2 * dd : 2 * dd + 2, :]
             return c
 
-        lax.fori_loop(0, order_local // 2, order, 0)
+        lax.fori_loop(0, order_local // UNROLL, order, 0)
         @pl.when(n + 2 < chunks)
         def _():
             coef_copy(n + 2).start()
 
         for i in range(half):
-            held[n, i] = four[mine + i].astype(BF16)
-            hsend[n, i] = four[theirs + i].astype(BF16)
+            held[n, i] = four[band(core, i)].astype(BF16)
+            hsend[n, i] = four[band(1 - core, i)].astype(BF16)
         pair_copy(n).start()
 
     def start_ring(n):
@@ -278,17 +286,17 @@
             i = lax.rem(sp + 2 + j, 4)
             partner_copy(n, i).start()
 
-            @pl.when(mine + i != sp)
+            @pl.when(band(core, i) != sp)
             def _():
                 own_copy(n, i).start()
 
-            @pl.when(mine + i == sp)
+            @pl.when(band(core, i) == sp)
             def _():
                 got[n, sp] = aown[n, i]
 
     def finish(n):
         for s in range(shards):
-            @pl.when(jnp.logical_or(s != sp, sp // half != core))
+            @pl.when(jnp.logical_or(s != sp, jnp.logical_not(mine_is)))
             def _():
                 arrival(n, s).wait_recv()
 
@@ -303,11 +311,10 @@
             res = jnp.dot(lhs, basis[:, lo : lo + 256], preferred_element_type=F32)
             for c in range(CB):
                 k = n * CB + c
-                old = field[k, :, lo : lo + width].astype(F32)
-                field[k, :, lo : lo + width] = (
+                old = out[0, k, :, lo : lo + width].astype(F32)
+                out[0, k, :, lo : lo + width] = (
                     old + scale[k] * res[32 * c : 32 * c + 32, :width]
                 ).astype(BF16)
-        out_copy(n).start()
 
     def tick(n, carry):
         def stage_at(lag, f):
@@ -315,18 +322,22 @@
             def _():
                 f(n - lag)
 
+        stage_at(1, start_ring)
+        stage_at(2, start_across)
+        stage_at(3, start_mean)
+        stage_at(4, start_exchange)
         stage_at(0, legendre)
-        stage_at(1, start_across)
-        stage_at(2, start_mean)
-        stage_at(3, start_exchange)
-        stage_at(0, start_ring)
-        stage_at(4, finish)
+
+        @pl.when(n == 2)
+        def _():
+            make_basis()
+
+        stage_at(5, finish)
         return carry
 
-    lax.fori_loop(0, chunks + 4, tick, 0)
+    lax.fori_loop(0, chunks + 5, tick, 0)
 
     def drain(n, carry):
-        out_copy(n).wait()
         pair_copy(n).wait_send()
         across_copy(n).wait_send()
         for j in range(1, 4):
@@ -335,13 +346,41 @@
         for i in range(half):
             partner_copy(n, i).wait_send()
 
-            @pl.when(mine + i != sp)
+            @pl.when(band(core, i) != sp)
             def _():
                 own_copy(n, i).wait_send()
 
         return carry
 
     lax.fori_loop(0, chunks, drain, 0)
+
+
+def hand_over(array):
+    pieces = 6
+    step = array.shape[1] // pieces
+
+    def body(src, dst, wsem):
+        def store(i):
+            part = pl.ds(i * step, step)
+            return pltpu.make_async_copy(src.at[0, part], dst.at[0, part], wsem.at[i])
+
+        for i in range(pieces):
+            store(i).start()
+        for i in range(pieces):
+            store(i).wait()
+
+    any_ = pl.BlockSpec(memory_space=pl.ANY)
+    return pl.pallas_call(
+        body,
+        out_shape=jax.ShapeDtypeStruct(array.shape, array.dtype),
+        in_specs=[pl.BlockSpec(memory_space=pltpu.VMEM)],
+        out_specs=any_,
+        scratch_shapes=[
+            pltpu.SemaphoreType.DMA((pieces,)),
+        ],
+        compiler_params=pltpu.CompilerParams(vmem_limit_bytes=20 * 1024 * 1024),
+        name="hand_over",
+    )(array)
 
 
 def local(weather, coefficients, channel_scale):
@@ -353,7 +392,7 @@
     chunks = channels // CB
     half = shards // 2
     factor = math.sqrt(3.0) * math.sqrt(4.0 * math.pi) / degrees * 2.0 ** (-30)
-    diag, angle, factors, wave = seeds(order_local, shards, lat, lat0, lon)
+    tables = seeds(order_local, shards, lat, lat0, lon)
     piece = (GR, 96, 128)
     V = pltpu.VMEM
     D = pltpu.SemaphoreType.DMA
@@ -361,11 +400,11 @@
     vmem = pl.BlockSpec(memory_space=pltpu.VMEM)
     smem = pl.BlockSpec(memory_space=pltpu.SMEM)
     dims = (chunks, order_local, degrees, lat, lon, shards, factor)
-    return pl.pallas_call(
+    result = pl.pallas_call(
         functools.partial(kernel, dims),
         out_shape=jax.ShapeDtypeStruct(weather.shape, weather.dtype),
-        in_specs=[any_, any_, smem, vmem, vmem, smem, vmem],
-        out_specs=any_,
+        in_specs=[any_, any_, smem, vmem],
+        out_specs=vmem,
         scratch_shapes=[
             V((2, CB, order_local, 2, degrees), jnp.int32),
             V((lat // 128, (order_local + 2) * 17, 128), F32),
@@ -385,8 +424,7 @@
             V((chunks, shards) + piece, BF16),
             V((96, 1536), F32),
             V((shards * 96, 1536), BF16),
-            V((channels, rows_local, lon), BF16),
-            D((2,)), D((chunks,)), D((chunks,)),
+            D((2,)), D((chunks,)),
             D((chunks,)), D((chunks,)),
             D((chunks, 3)), D((chunks, 3)),
             D((chunks,)), D((chunks,)),
@@ -394,10 +432,11 @@
             D((chunks, half)), D((chunks, half)), D((chunks, shards)),
         ],
         compiler_params=pltpu.CompilerParams(
-            collective_id=0, has_side_effects=True, vmem_limit_bytes=67043328
+            collective_id=0, has_side_effects=True, vmem_limit_bytes=44 * 1024 * 1024
         ),
         name="synthesis",
-    )(weather, coefficients.transpose(0, 1, 3, 2, 4), channel_scale, diag, angle, factors, wave)
+    )(weather, coefficients.transpose(0, 1, 3, 2, 4), channel_scale, tables)
+    return hand_over(result)
 
 
 def solution(mesh):

time: 120 us -> 98.3 us (0.82)
  Pallas kernels: 112 us -> 96.3 us
  local copies, waits for them, and re-layouts: 7.72 us -> 1.89 us
    pallas_call x1, Pallas kernels: 112 us -> 92.9 us  [local(): pl.pallas_call(functools.partial(kernel, dims), out_shape=jax.ShapeDtypeS...]
    unnamed x1 -> x4, local copies, waits for them, and re-layouts: 7.72 us -> 1.89 us
    pallas_call x0 -> x1, Pallas kernels: none -> 3.36 us  [hand_over(): pl.pallas_call(body, out_shape=jax.ShapeDtypeStruct(array.shape, array.dt...]
where the time goes in v2:
time: 98.3 us; the launch traced here: 98.2 us
  Pallas kernels  96.3 us (98%)
  local copies, waits for them, and re-layouts  1.89 us (2%)
    pallas_call x1, Pallas kernels, local(): pl.pallas_call(functools.partial(kernel, dims), out_shape=jax.ShapeDtypeS...  92.9 us
    pallas_call x1, Pallas kernels, hand_over(): pl.pallas_call(body, out_shape=jax.ShapeDtypeStruct(array.shape, array.dt...  3.36 us

profile of v2, /device:TPU:0, one launch (start us, length us, event | category | flops | bytes accessed | tf_op | source)
XLA Modules:
  0.0 98.2 jit_solution(17165191836377527408)
XLA Ops:
  0.0 0.0 copy-start
  0.0 1.2 %copy-done = f32[176,1536]{1,0:T(8,128)S(1)} copy-done((f32[176,1536]{1,0:T(8,128)S(1)}, f32[176,1536]{1,0:T(8,128)}, u32[]{:S(2)}) %copy-start) | copy-done | bytes 1081368
  1.2 0.0 copy-start.1
  1.2 0.7 copy-done.1
  1.9 92.9 %synthesis.1.src = bf16[1,84,32,1440]{3,2,1,0:T(8,128)(2,1)S(1)} custom-call(bf16[1,84,32,1440]{3,2,1,0:T(8,128)(2,1)} %weather.1, s32[1,84,46,2,361]{4,3,2,1,0:T(2,128)} %bitcast.1, f32[84]{0:T(128)S(1)} %copy-done.1, f32[176,1536]{1,0:T(8,128)S(1)} %copy-done), custom_call_target="tpu_custom_call" | custom-call | tf_op jit(solution)/shard_map/synthesis/pallas_call | solution.py:403
  94.8 3.4 %hand_over.1 = bf16[1,84,32,1440]{3,2,1,0:T(8,128)(2,1)} custom-call(bf16[1,84,32,1440]{3,2,1,0:T(8,128)(2,1)S(1)} %synthesis.1.src), custom_call_target="tpu_custom_call" | custom-call | tf_op jit(solution)/shard_map/hand_over/pallas_call | solution.py:373
Async XLA Ops:
  0.0 1.2 %copy-start = (f32[176,1536]{1,0:T(8,128)S(1)}, f32[176,1536]{1,0:T(8,128)}, u32[]{:S(2)}) copy-start(f32[176,1536]{1,0:T(8,128)} %constant.2.clone.tables) | copy-start | bytes 3244036
  1.2 0.7 copy-start.1

commit v3 on v2

--- a/solution.py
+++ b/solution.py
@@ -16,6 +16,7 @@
 GR = CB // 4
 LPAD = 384
 UNROLL = 23
+EARLY = 1
 
 
 def seeds(order_local, shards, lat, lat0, lon):
@@ -58,8 +59,8 @@
 def kernel(
     dims, weather, coefs, scale, tables, out,
     cbuf, stage, table, four, held, hsend, hrecv, zsend, zrecv, xsend, xrecv,
-    msend, mrecv, aown, apar, got, rows, basis,
-    csem, wsem, hs, hr, zs, zr, xs, xr, ms, mr, sown, spar, ar,
+    msend, mrecv, aown, apar, got, back, rows, basis,
+    csem, wsem, hs, hr, zs, zr, xs, xr, ms, mr, sown, spar, ar, hs4, hr4, bs, br,
 ):
     chunks, order_local, degrees, lat, lon, shards, factor = dims
     half = shards // 2
@@ -219,6 +220,71 @@
             device_id=(other, sp), device_id_type=MESH,
         )
 
+    def early(n):
+        return jnp.logical_and(lax.rem(n, 2) == 0, n < EARLY)
+
+    def raw_near(n, i):
+        return pltpu.make_async_remote_copy(
+            held.at[n, i], got.at[n, sp], sown.at[n, i], ar.at[n, sp],
+            device_id=(me, band(core, i)), device_id_type=MESH,
+        )
+
+    def raw_far(n, i):
+        return pltpu.make_async_remote_copy(
+            hsend.at[n, i], got.at[n, sp], spar.at[n, i], ar.at[n, sp],
+            device_id=(me, band(1 - core, i)), device_id_type=MESH,
+        )
+
+    def piece_copy(n, i):
+        return pltpu.make_async_remote_copy(
+            got.at[n, band(1 - core, i)], hrecv.at[n, i], hs4.at[n, i], hr4.at[n, i],
+            device_id=(other, sp), device_id_type=MESH,
+        )
+
+    def return_copy(n, i):
+        return pltpu.make_async_remote_copy(
+            apar.at[n, i], back.at[n // 2, i], bs.at[n, i], br.at[n, i],
+            device_id=(other, sp), device_id_type=MESH,
+        )
+
+    def start_pieces(n):
+        for s in range(shards):
+            @pl.when(s != sp)
+            def _():
+                arrival(n, s).wait_recv()
+
+        for i in range(half):
+            piece_copy(n, i).start()
+
+    def start_early_ring(n):
+        for i in range(half):
+            piece_copy(n, i).wait_recv()
+            total = got[n, band(core, i)].astype(F32) + hrecv[n, i].astype(F32)
+            zsend[n, i] = total.astype(BF16)
+        for j in (2, 1, 3):
+            ring_copy(n, j).start()
+
+    def start_return(n):
+        for j in range(4):
+            i = lax.rem(zpos - j + 4, 4)
+            if j == 0:
+                mean = msend[n].astype(F32)
+            else:
+                mean_copy(n, j).wait_recv()
+                mean = mrecv[n, j - 1].astype(F32)
+            at = band(core, i)
+            got[n, at] = (got[n, at].astype(F32) - mean).astype(BF16)
+            apar[n, i] = (hrecv[n, i].astype(F32) - mean).astype(BF16)
+        for i in range(half):
+            return_copy(n, i).start()
+
+    def finish_early(n):
+        for i in range(half):
+            return_copy(n, i).wait_recv()
+            piece_copy(n, i).wait_send()
+            got[n, band(1 - core, i)] = back[n // 2, i]
+        transform(n)
+
     def legendre(n):
         slot = lax.rem(n, 2)
         coef_copy(n).wait()
@@ -248,7 +314,26 @@
         for i in range(half):
             held[n, i] = four[band(core, i)].astype(BF16)
             hsend[n, i] = four[band(1 - core, i)].astype(BF16)
-        pair_copy(n).start()
+
+        @pl.when(jnp.logical_not(early(n)))
+        def _():
+            pair_copy(n).start()
+
+        @pl.when(early(n))
+        def _():
+            for j in range(half):
+                i = lax.rem(sp + 2 + j, half)
+                for raw, to, src in (
+                    (raw_far, band(1 - core, i), hsend),
+                    (raw_near, band(core, i), held),
+                ):
+                    @pl.when(to != sp)
+                    def _():
+                        raw(n, i).start()
+
+                    @pl.when(to == sp)
+                    def _():
+                        got[n, sp] = src[n, i]
 
     def start_ring(n):
         pair_copy(n).wait_recv()
@@ -300,6 +385,9 @@
             def _():
                 arrival(n, s).wait_recv()
 
+        transform(n)
+
+    def transform(n):
         weather_copy(n).wait()
         lhs = []
         for g in range(GR):
@@ -317,38 +405,65 @@
                 ).astype(BF16)
 
     def tick(n, carry):
-        def stage_at(lag, f):
-            @pl.when(jnp.logical_and(n >= lag, n < chunks + lag))
+        def stage_at(lag, f, kind=None):
+            k = n - lag
+            on = jnp.logical_and(k >= 0, k < chunks)
+            if kind is not None:
+                on = jnp.logical_and(on, early(k) if kind else jnp.logical_not(early(k)))
+
+            @pl.when(on)
             def _():
-                f(n - lag)
-
-        stage_at(1, start_ring)
-        stage_at(2, start_across)
-        stage_at(3, start_mean)
-        stage_at(4, start_exchange)
+                f(k)
+
+        stage_at(1, start_ring, False)
+        stage_at(6, start_early_ring, True)
+        stage_at(2, start_across, False)
+        stage_at(7, start_across, True)
+        stage_at(3, start_mean, False)
+        stage_at(8, start_mean, True)
+        stage_at(4, start_exchange, False)
+        stage_at(9, start_return, True)
         stage_at(0, legendre)
 
         @pl.when(n == 2)
         def _():
             make_basis()
 
-        stage_at(5, finish)
+        stage_at(5, start_pieces, True)
+        stage_at(5, finish, False)
+        stage_at(10, finish_early, True)
         return carry
 
-    lax.fori_loop(0, chunks + 5, tick, 0)
+    lax.fori_loop(0, max(chunks + 5, EARLY + 10), tick, 0)
 
     def drain(n, carry):
-        pair_copy(n).wait_send()
         across_copy(n).wait_send()
         for j in range(1, 4):
             ring_copy(n, j).wait_send()
             mean_copy(n, j).wait_send()
-        for i in range(half):
-            partner_copy(n, i).wait_send()
-
-            @pl.when(band(core, i) != sp)
-            def _():
-                own_copy(n, i).wait_send()
+
+        @pl.when(jnp.logical_not(early(n)))
+        def _():
+            pair_copy(n).wait_send()
+            for i in range(half):
+                partner_copy(n, i).wait_send()
+
+                @pl.when(band(core, i) != sp)
+                def _():
+                    own_copy(n, i).wait_send()
+
+        @pl.when(early(n))
+        def _():
+            for i in range(half):
+                return_copy(n, i).wait_send()
+
+                @pl.when(band(core, i) != sp)
+                def _():
+                    raw_near(n, i).wait_send()
+
+                @pl.when(band(1 - core, i) != sp)
+                def _():
+                    raw_far(n, i).wait_send()
 
         return carry
 
@@ -422,6 +537,7 @@
             V((chunks, half) + piece, BF16),
             V((chunks, half) + piece, BF16),
             V((chunks, shards) + piece, BF16),
+            V(((EARLY + 1) // 2, half) + piece, BF16),
             V((96, 1536), F32),
             V((shards * 96, 1536), BF16),
             D((2,)), D((chunks,)),
@@ -430,6 +546,7 @@
             D((chunks,)), D((chunks,)),
             D((chunks, 3)), D((chunks, 3)),
             D((chunks, half)), D((chunks, half)), D((chunks, shards)),
+            D((chunks, half)), D((chunks, half)), D((chunks, half)), D((chunks, half)),
         ],
         compiler_params=pltpu.CompilerParams(
             collective_id=0, has_side_effects=True, vmem_limit_bytes=44 * 1024 * 1024

time: 98.3 us -> 95.4 us (0.970)
  Pallas kernels: 96.3 us -> 93.3 us
    pallas_call x1, Pallas kernels: 92.9 us -> 90 us  [local(): pl.pallas_call(functools.partial(kernel, dims), out_shape=jax.ShapeDtypeS...]
where the time goes in v3:
time: 95.4 us; the launch traced here: 95.2 us
  Pallas kernels  93.3 us (98%)
  local copies, waits for them, and re-layouts  1.89 us (2%)
    pallas_call x1, Pallas kernels, local(): pl.pallas_call(functools.partial(kernel, dims), out_shape=jax.ShapeDtypeS...  90 us
    pallas_call x1, Pallas kernels, hand_over(): pl.pallas_call(body, out_shape=jax.ShapeDtypeStruct(array.shape, array.dt...  3.36 us

profile of v3, /device:TPU:0, one launch (start us, length us, event | category | flops | bytes accessed | tf_op | source)
XLA Modules:
  0.0 95.2 jit_solution(3521991741289870736)
XLA Ops:
  0.0 0.0 copy-start
  0.0 1.2 %copy-done = f32[176,1536]{1,0:T(8,128)S(1)} copy-done((f32[176,1536]{1,0:T(8,128)S(1)}, f32[176,1536]{1,0:T(8,128)}, u32[]{:S(2)}) %copy-start) | copy-done | bytes 1081368
  1.2 0.0 copy-start.1
  1.2 0.7 copy-done.1
  1.9 90.0 %synthesis.1.src = bf16[1,84,32,1440]{3,2,1,0:T(8,128)(2,1)S(1)} custom-call(bf16[1,84,32,1440]{3,2,1,0:T(8,128)(2,1)} %weather.1, s32[1,84,46,2,361]{4,3,2,1,0:T(2,128)} %bitcast.1, f32[84]{0:T(128)S(1)} %copy-done.1, f32[176,1536]{1,0:T(8,128)S(1)} %copy-done), custom_call_target="tpu_custom_call" | custom-call | tf_op jit(solution)/shard_map/synthesis/pallas_call | solution.py:518
  91.9 3.4 %hand_over.1 = bf16[1,84,32,1440]{3,2,1,0:T(8,128)(2,1)} custom-call(bf16[1,84,32,1440]{3,2,1,0:T(8,128)(2,1)S(1)} %synthesis.1.src), custom_call_target="tpu_custom_call" | custom-call | tf_op jit(solution)/shard_map/hand_over/pallas_call | solution.py:488
Async XLA Ops:
  0.0 1.2 %copy-start = (f32[176,1536]{1,0:T(8,128)S(1)}, f32[176,1536]{1,0:T(8,128)}, u32[]{:S(2)}) copy-start(f32[176,1536]{1,0:T(8,128)} %constant.2.clone.tables) | copy-start | bytes 3244036
  1.2 0.7 copy-start.1
